TPU v7x, 32 devices: a whole 2x2x4 slice. The times are simulated.
32 devices in a mesh: grp: 4 (over z), slab: 8 (over y, x, core).
Axes of the slice: x: 2, y: 2, z: 4, core: 2. Of those that a mesh axis runs over, the one named last changes fastest.
Arguments:
- tensor: float32 [672, 64, 672], P('grp', 'slab'), may hold values from -20 to 20
- start_one: float32 [672, 96], replicated, may hold values from -6 to 6
- start_two: float32 [672, 96], replicated, may hold values from -6 to 6
Outputs:
- basis_one: float32 [672, 96], replicated
- basis_two: float32 [672, 96], replicated
- core: float32 [96, 64, 96], P('grp', 'slab')
All inputs are finite; a program needn't handle non-finite values.
Results may differ from a plain program's by a relative error of at most 0.0003.
Values sent between devices are 32-bit elements; how exact they have to be, the bound alone decides.
No kernel may reach another device: no remote copies, remote signals or barrier semaphores. Data moves between devices by JAX's collectives and lax.ppermute only.
A program may use at most 64 MiB of HBM per device.

v0:
```python
import jax
import jax.numpy as jnp
from jax import lax
from jax.sharding import PartitionSpec as P

ITERS = 2
HIGH = lax.Precision.HIGHEST


def orthonormal(widened):
    cross = jnp.dot(widened.T, widened, precision=HIGH)
    lower_small = jnp.linalg.cholesky(cross)
    return lax.linalg.triangular_solve(
        lower_small, widened, left_side=False, lower=True, transpose_a=True
    )


def iterate_basis(gram, start):
    current = start
    for _ in range(ITERS):
        current = orthonormal(jnp.dot(gram, current, precision=HIGH))
    return current


def local(tensor, start_one, start_two):
    block_gram = jnp.einsum("jmi,jmk->ik", tensor, tensor, precision=HIGH)
    gram_one = lax.psum(block_gram, ("grp", "slab"))
    basis_one = iterate_basis(gram_one, start_one)
    reduced = jnp.einsum("jmi,ia->jma", tensor, basis_one, precision=HIGH)
    regrouped = lax.all_to_all(reduced, "grp", split_axis=1, concat_axis=0, tiled=True)
    block_second = jnp.einsum("jma,kma->jk", regrouped, regrouped, precision=HIGH)
    gram_two = lax.psum(block_second, ("grp", "slab"))
    basis_two = iterate_basis(gram_two, start_two)
    core_block = jnp.einsum("jb,jma->bma", basis_two, regrouped, precision=HIGH)
    core = lax.all_to_all(core_block, "grp", split_axis=0, concat_axis=1, tiled=True)
    return (basis_one, basis_two, core)


def solution(mesh):
    in_specs = (P("grp", "slab", None), P(), P())
    out_specs = (P(), P(), P("grp", "slab", None))
    return jax.shard_map(local, mesh=mesh, in_specs=in_specs, out_specs=out_specs, check_vma=False)
```

profile of v0, /device:TPU:0, one launch (start us, length us, event | category | flops | bytes accessed | tf_op | source)
XLA Modules:
  0.0 439.0 jit_solution(15188821805483427743)
XLA Ops:
  7.2 18.1 %fusion.4 = f32[672,672]{1,0:T(8,128)} fusion(f32[168,8,672]{2,1,0:T(8,128)} %param.6), kind=kOutput, calls=%fused_computation.5 | convolution fusion | flops 7283146752 | bytes 5419008 | tf_op jit(solution)/shard_map/jmi,jmk->ik/dot_general | solution.py:26
  25.8 136.7 %all-reduce.3.cloned.1.call-done = f32[672,672]{1,0:T(8,128)} async-done(((f32[672,672]{1,0:T(8,128)}), f32[672,672]{1,0:T(8,128)}) %all-reduce.3.cloned.1.call-update) | async-done | bytes 1806352 | tf_op jit(solution)/shard_map/psum | solution.py:27
  162.4 3.7 fusion.29
  166.6 8.8 %cholesky.74 = f32[96,96]{1,0:T(8,128)S(1)} custom-call(f32[96,96]{1,0:T(8,128)S(1)} %fusion.26), custom_call_target="Cholesky" | custom-call | tf_op jit(solution)/shard_map/jit(cholesky)/cholesky | solution.py:12
  175.4 0.6 compare_reduce_fusion.3
  176.1 0.7 fusion.13
  176.7 7.4 %custom-call.8 = f32[1,96,96]{1,2,0:T(8,128)S(1)} custom-call(f32[1,96,96]{2,1,0:T(8,128)S(1)} %fusion.13), custom_call_target="InvertDiagBlocksLowerTriangular" | custom-call | tf_op jit(solution)/shard_map/triangular_solve/custom-call.0 | solution.py:13
  184.1 0.4 convolution_bitcast_fusion.2
  184.6 2.0 fusion.31
  187.0 8.8 %cholesky.85 = f32[96,96]{1,0:T(8,128)S(1)} custom-call(f32[96,96]{1,0:T(8,128)S(1)} %fusion.24), custom_call_target="Cholesky" | custom-call | tf_op jit(solution)/shard_map/jit(cholesky)/cholesky | solution.py:12
  195.9 0.6 compare_reduce_fusion.2
  196.5 0.7 fusion.14
  197.2 7.4 %custom-call.9 = f32[1,96,96]{1,2,0:T(8,128)S(1)} custom-call(f32[1,96,96]{2,1,0:T(8,128)S(1)} %fusion.14), custom_call_target="InvertDiagBlocksLowerTriangular" | custom-call | tf_op jit(solution)/shard_map/triangular_solve/custom-call.0 | solution.py:13
  205.0 17.6 %fusion.7 = f32[168,8,96]{2,0,1:T(8,128)S(1)} fusion(f32[168,8,672]{2,1,0:T(8,128)} %param.6, f32[96,672]{1,0:T(8,128)S(1)} %fusion.22), kind=kOutput, calls=%fused_computation.6 | convolution fusion | flops 1040449536 | bytes 4386816 | tf_op jit(solution)/shard_map/jmi,ia->jma/dot_general | solution.py:29
  222.7 19.8 %all_to_all.36 = f32[168,8,96]{2,0,1:T(8,128)S(1)} all-to-all(f32[168,8,96]{2,0,1:T(8,128)S(1)} %fusion.7), channel_id=1, replica_groups=mesh['grp'=4,'slab'=8] {'grp'}, dimensions={1} | all-to-all | bytes 1032192 | tf_op jit(solution)/shard_map/all_to_all | solution.py:30
  242.5 3.1 convolution_bitcast_fusion
  245.6 133.2 %all-reduce.5.cloned.1.call-done = f32[672,672]{1,0:T(8,128)} async-done(((f32[672,672]{1,0:T(8,128)}), f32[672,672]{1,0:T(8,128)}) %all-reduce.5.cloned.1.call-update) | async-done | bytes 1806352 | tf_op jit(solution)/shard_map/psum | solution.py:32
  378.8 3.7 fusion.33
  383.0 8.8 %cholesky.96 = f32[96,96]{1,0:T(8,128)S(1)} custom-call(f32[96,96]{1,0:T(8,128)S(1)} %fusion.21), custom_call_target="Cholesky" | custom-call | tf_op jit(solution)/shard_map/jit(cholesky)/cholesky | solution.py:12
  391.8 0.6 compare_reduce_fusion.1
  392.4 0.7 fusion.15
  393.1 7.4 %custom-call.10 = f32[1,96,96]{1,2,0:T(8,128)S(1)} custom-call(f32[1,96,96]{2,1,0:T(8,128)S(1)} %fusion.15), custom_call_target="InvertDiagBlocksLowerTriangular" | custom-call | tf_op jit(solution)/shard_map/triangular_solve/custom-call.0 | solution.py:13
  400.5 0.4 convolution_bitcast_fusion.1
  400.9 2.0 fusion.35
  403.4 8.9 %cholesky.107 = f32[96,96]{1,0:T(8,128)S(1)} custom-call(f32[96,96]{1,0:T(8,128)S(1)} %fusion.19), custom_call_target="Cholesky" | custom-call | tf_op jit(solution)/shard_map/jit(cholesky)/cholesky | solution.py:12
  412.3 0.6 compare_reduce_fusion
  413.0 0.7 fusion.16
  413.6 7.4 %custom-call.11 = f32[1,96,96]{1,2,0:T(8,128)S(1)} custom-call(f32[1,96,96]{2,1,0:T(8,128)S(1)} %fusion.16), custom_call_target="InvertDiagBlocksLowerTriangular" | custom-call | tf_op jit(solution)/shard_map/triangular_solve/custom-call.0 | solution.py:13
  421.0 0.4 fusion.17
  421.5 0.5 fusion.10
  422.0 9.2 %all_to_all.37 = f32[96,2,96]{2,1,0:T(2,128)S(1)} all-to-all(f32[96,2,96]{2,1,0:T(2,128)S(1)} %copy.38), channel_id=1, replica_groups=mesh['grp'=4,'slab'=8] {'grp'}, dimensions={0} | all-to-all | bytes 147456 | tf_op jit(solution)/shard_map/all_to_all | solution.py:35
  431.3 0.7 copy.39
  (33 shorter events, 3.2 us)
Async XLA Ops:
  7.2 155.3 %copy-start = (f32[672,96]{0,1:T(8,128)S(1)}, f32[672,96]{0,1:T(8,128)}, u32[]{:S(2)}) copy-start(f32[672,96]{0,1:T(8,128)} %param.7) | copy-start | bytes 774148
  7.2 155.2 %all-reduce.3.cloned.1.call-start = ((), (), s32[]{:S(2)}) async-start(), calls=%async_computation.2 | async-start | bytes 4128768 | tf_op jit(solution)/shard_map/psum | solution.py:27
  25.3 353.5 %all-reduce.5.cloned.1.call-start = ((), (), s32[]{:S(2)}) async-start(), calls=%async_computation.3 | async-start | bytes 4128768 | tf_op jit(solution)/shard_map/psum | solution.py:32
  162.4 22.1 %copy-start.1 = (f32[672,672]{1,0:T(8,128)S(1)}, f32[672,672]{1,0:T(8,128)}, u32[]{:S(2)}) copy-start(f32[672,672]{1,0:T(8,128)} %all-reduce.3.cloned.1.call-done) | copy-start | bytes 5419012
  205.0 17.7 %copy-start.3 = (f32[96,672]{1,0:T(8,128)}, f32[96,672]{1,0:T(8,128)S(1)}, u32[]{:S(2)}) copy-start(f32[96,672]{1,0:T(8,128)S(1)} %fusion.22) | copy-start | bytes 774148
  378.8 22.1 %copy-start.2 = (f32[672,672]{1,0:T(8,128)S(1)}, f32[672,672]{1,0:T(8,128)}, u32[]{:S(2)}) copy-start(f32[672,672]{1,0:T(8,128)} %all-reduce.5.cloned.1.call-done) | copy-start | bytes 5419012
  421.4 10.5 %copy-start.4 = (f32[96,672]{1,0:T(8,128)}, f32[96,672]{1,0:T(8,128)S(1)}, u32[]{:S(2)}) copy-start(f32[96,672]{1,0:T(8,128)S(1)} %fusion.17) | copy-start | bytes 774148
Sparse Core Ops, SparseCore 0:
  25.4 136.9 all-reduce.2
  245.7 133.0 all-reduce.4
where the time goes:
time: 445 us; the launch traced here: 439 us
  waiting for transfers between devices  270 us (61%)
  other arithmetic  70 us (16%)
  matrix products  53.9 us (12%)
  blocking collectives  29 us (7%)
  between operations  14.6 us (3%)
    psum x1, waiting for transfers between devices, local(): gram_one = lax.psum(block_gram, ('grp', 'slab'))  137 us
    psum x1, waiting for transfers between devices, local(): gram_two = lax.psum(block_second, ('grp', 'slab'))  133 us
    another operation x12, other arithmetic, orthonormal(): lower_small = jnp.linalg.cholesky(cross)  37.9 us
    another operation x8, other arithmetic, orthonormal(): lax.linalg.triangular_solve(lower_small, widened, left_side=False, lower=...  32 us
    all_to_all x1, blocking collectives, local(): lax.all_to_all(reduced, 'grp', split_axis=1, concat_axis=0, tiled=True)  19.8 us
    dot_general x1, matrix products, local(): block_gram = jnp.einsum('jmi,jmk->ik', tensor, tensor, precision=HIGH)  18.1 us
    dot_general x1, matrix products, local(): reduced = jnp.einsum('jmi,ia->jma', tensor, basis_one, precision=HIGH)  17.6 us
    dot_general x4, matrix products, iterate_basis(): current = orthonormal(jnp.dot(gram, current, precision=HIGH))  11.3 us
  transfers between devices with their start and end apart: 2, of which 2 were waited for; matrix products, arithmetic and copies ran while one was open for 0% of the time, Pallas kernels for 0%

commit v1 on v0

--- a/solution.py
+++ b/solution.py
@@ -24,7 +24,13 @@
 
 def local(tensor, start_one, start_two):
     block_gram = jnp.einsum("jmi,jmk->ik", tensor, tensor, precision=HIGH)
-    gram_one = lax.psum(block_gram, ("grp", "slab"))
+
+    def lift_object(bus_axis, t0, a_name):
+        for src_i in (bus_axis, a_name):
+            t0 = jax.lax.psum(t0, src_i)
+        return t0
+
+    gram_one = lift_object("slab", block_gram, "grp")
     basis_one = iterate_basis(gram_one, start_one)
     reduced = jnp.einsum("jmi,ia->jma", tensor, basis_one, precision=HIGH)
     regrouped = lax.all_to_all(reduced, "grp", split_axis=1, concat_axis=0, tiled=True)

time: 445 us -> 460 us (1.034)
  waiting for transfers between devices: 270 us -> 284 us
    psum x1 -> x2, waiting for transfers between devices: 137 us -> 151 us  [lift_object(): t0 = jax.lax.psum(t0, src_i)]
  transfers between devices with their start and end apart: 2 -> 3, of which waited for: 2 -> 3; matrix products, arithmetic and copies ran while one was open for 0% -> 0% of each run, Pallas kernels for 0% -> 0%
where the time goes in v1:
time: 460 us; the launch traced here: 454 us
  waiting for transfers between devices  284 us (62%)
  other arithmetic  70 us (15%)
  matrix products  53.9 us (12%)
  blocking collectives  30.1 us (7%)
  between operations  14.3 us (3%)
    psum x2, waiting for transfers between devices, lift_object(): t0 = jax.lax.psum(t0, src_i)  151 us
    psum x1, waiting for transfers between devices, local(): gram_two = lax.psum(block_second, ('grp', 'slab'))  133 us
    another operation x12, other arithmetic, orthonormal(): lower_small = jnp.linalg.cholesky(cross)  37.9 us
    another operation x8, other arithmetic, orthonormal(): lax.linalg.triangular_solve(lower_small, widened, left_side=False, lower=...  32 us
    all_to_all x1, blocking collectives, local(): lax.all_to_all(reduced, 'grp', split_axis=1, concat_axis=0, tiled=True)  20.9 us
    dot_general x1, matrix products, local(): block_gram = jnp.einsum('jmi,jmk->ik', tensor, tensor, precision=HIGH)  18.1 us
    dot_general x1, matrix products, local(): reduced = jnp.einsum('jmi,ia->jma', tensor, basis_one, precision=HIGH)  17.6 us
    dot_general x4, matrix products, iterate_basis(): current = orthonormal(jnp.dot(gram, current, precision=HIGH))  11.3 us
  transfers between devices with their start and end apart: 3, of which 3 were waited for; matrix products, arithmetic and copies ran while one was open for 0% of the time, Pallas kernels for 0%

profile of v1, /device:TPU:0, one launch (start us, length us, event | category | flops | bytes accessed | tf_op | source)
XLA Modules:
  0.0 453.9 jit_solution(18090042723905139410)
XLA Ops:
  7.2 18.1 %fusion.4 = f32[672,672]{1,0:T(8,128)} fusion(f32[168,8,672]{2,1,0:T(8,128)} %param.6), kind=kOutput, calls=%fused_computation.5 | convolution fusion | flops 7283146752 | bytes 5419008 | tf_op jit(solution)/shard_map/jmi,jmk->ik/dot_general | solution.py:26
  25.4 64.5 %all-reduce.4.cloned.1.call-done = f32[672,672]{1,0:T(8,128)} async-done(((f32[672,672]{1,0:T(8,128)}), f32[672,672]{1,0:T(8,128)}) %all-reduce.4.cloned.1.call-update) | async-done | bytes 1806352 | tf_op jit(solution)/shard_map/psum | solution.py:30
  90.3 86.2 %all-reduce.6.cloned.1.call-done = f32[672,672]{1,0:T(8,128)} async-done(((f32[672,672]{1,0:T(8,128)}), f32[672,672]{1,0:T(8,128)}) %all-reduce.6.cloned.1.call-update) | async-done | bytes 1806352 | tf_op jit(solution)/shard_map/psum | solution.py:30
  176.6 3.7 fusion.29
  180.8 8.8 %cholesky.74 = f32[96,96]{1,0:T(8,128)S(1)} custom-call(f32[96,96]{1,0:T(8,128)S(1)} %fusion.26), custom_call_target="Cholesky" | custom-call | tf_op jit(solution)/shard_map/jit(cholesky)/cholesky | solution.py:12
  189.6 0.6 compare_reduce_fusion.3
  190.2 0.7 fusion.13
  190.9 7.4 %custom-call.8 = f32[1,96,96]{1,2,0:T(8,128)S(1)} custom-call(f32[1,96,96]{2,1,0:T(8,128)S(1)} %fusion.13), custom_call_target="InvertDiagBlocksLowerTriangular" | custom-call | tf_op jit(solution)/shard_map/triangular_solve/custom-call.0 | solution.py:13
  198.7 2.0 fusion.31
  201.2 8.8 %cholesky.85 = f32[96,96]{1,0:T(8,128)S(1)} custom-call(f32[96,96]{1,0:T(8,128)S(1)} %fusion.24), custom_call_target="Cholesky" | custom-call | tf_op jit(solution)/shard_map/jit(cholesky)/cholesky | solution.py:12
  210.0 0.6 compare_reduce_fusion.2
  210.6 0.7 fusion.14
  211.3 7.4 %custom-call.9 = f32[1,96,96]{1,2,0:T(8,128)S(1)} custom-call(f32[1,96,96]{2,1,0:T(8,128)S(1)} %fusion.14), custom_call_target="InvertDiagBlocksLowerTriangular" | custom-call | tf_op jit(solution)/shard_map/triangular_solve/custom-call.0 | solution.py:13
  218.7 0.4 fusion.22
  219.1 17.6 %fusion.7 = f32[168,8,96]{2,0,1:T(8,128)S(1)} fusion(f32[168,8,672]{2,1,0:T(8,128)} %param.6, f32[96,672]{1,0:T(8,128)S(1)} %fusion.22), kind=kOutput, calls=%fused_computation.6 | convolution fusion | flops 1040449536 | bytes 4386816 | tf_op jit(solution)/shard_map/jmi,ia->jma/dot_general | solution.py:35
  236.8 20.9 %all_to_all.36 = f32[168,8,96]{2,0,1:T(8,128)S(1)} all-to-all(f32[168,8,96]{2,0,1:T(8,128)S(1)} %fusion.7), channel_id=1, replica_groups=mesh['grp'=4,'slab'=8] {'grp'}, dimensions={1} | all-to-all | bytes 1032192 | tf_op jit(solution)/shard_map/all_to_all | solution.py:36
  257.7 3.1 convolution_bitcast_fusion
  260.8 133.2 %all-reduce.8.cloned.1.call-done = f32[672,672]{1,0:T(8,128)} async-done(((f32[672,672]{1,0:T(8,128)}), f32[672,672]{1,0:T(8,128)}) %all-reduce.8.cloned.1.call-update) | async-done | bytes 1806352 | tf_op jit(solution)/shard_map/psum | solution.py:38
  394.0 3.7 fusion.33
  398.2 8.8 %cholesky.96 = f32[96,96]{1,0:T(8,128)S(1)} custom-call(f32[96,96]{1,0:T(8,128)S(1)} %fusion.21), custom_call_target="Cholesky" | custom-call | tf_op jit(solution)/shard_map/jit(cholesky)/cholesky | solution.py:12
  407.0 0.6 compare_reduce_fusion.1
  407.6 0.7 fusion.15
  408.3 7.4 %custom-call.10 = f32[1,96,96]{1,2,0:T(8,128)S(1)} custom-call(f32[1,96,96]{2,1,0:T(8,128)S(1)} %fusion.15), custom_call_target="InvertDiagBlocksLowerTriangular" | custom-call | tf_op jit(solution)/shard_map/triangular_solve/custom-call.0 | solution.py:13
  415.7 0.4 convolution_bitcast_fusion.1
  416.1 2.0 fusion.35
  418.6 8.9 %cholesky.107 = f32[96,96]{1,0:T(8,128)S(1)} custom-call(f32[96,96]{1,0:T(8,128)S(1)} %fusion.19), custom_call_target="Cholesky" | custom-call | tf_op jit(solution)/shard_map/jit(cholesky)/cholesky | solution.py:12
  427.5 0.6 compare_reduce_fusion
  428.2 0.7 fusion.16
  428.8 7.4 %custom-call.11 = f32[1,96,96]{1,2,0:T(8,128)S(1)} custom-call(f32[1,96,96]{2,1,0:T(8,128)S(1)} %fusion.16), custom_call_target="InvertDiagBlocksLowerTriangular" | custom-call | tf_op jit(solution)/shard_map/triangular_solve/custom-call.0 | solution.py:13
  436.7 0.5 fusion.10
  437.2 9.2 %all_to_all.37 = f32[96,2,96]{2,1,0:T(2,128)S(1)} all-to-all(f32[96,2,96]{2,1,0:T(2,128)S(1)} %copy.38), channel_id=1, replica_groups=mesh['grp'=4,'slab'=8] {'grp'}, dimensions={0} | all-to-all | bytes 147456 | tf_op jit(solution)/shard_map/all_to_all | solution.py:41
  446.5 0.7 copy.39
  (36 shorter events, 3.6 us)
Async XLA Ops:
  7.2 169.4 %copy-start = (f32[672,96]{0,1:T(8,128)S(1)}, f32[672,96]{0,1:T(8,128)}, u32[]{:S(2)}) copy-start(f32[672,96]{0,1:T(8,128)} %param.7) | copy-start | bytes 774148
  7.2 82.7 %all-reduce.4.cloned.1.call-start = ((), (), s32[]{:S(2)}) async-start(), calls=%async_computation.2 | async-start | bytes 4128768 | tf_op jit(solution)/shard_map/psum | solution.py:30
  25.3 151.2 %all-reduce.6.cloned.1.call-start = ((), (), s32[]{:S(2)}) async-start(), calls=%async_computation.3 | async-start | bytes 4128768 | tf_op jit(solution)/shard_map/psum | solution.py:30
  89.9 304.1 %all-reduce.8.cloned.1.call-start = ((), (), s32[]{:S(2)}) async-start(), calls=%async_computation.4 | async-start | bytes 4128768 | tf_op jit(solution)/shard_map/psum | solution.py:38
  176.6 22.1 %copy-start.1 = (f32[672,672]{1,0:T(8,128)S(1)}, f32[672,672]{1,0:T(8,128)}, u32[]{:S(2)}) copy-start(f32[672,672]{1,0:T(8,128)} %all-reduce.6.cloned.1.call-done) | copy-start | bytes 5419012
  219.1 17.7 %copy-start.3 = (f32[96,672]{1,0:T(8,128)}, f32[96,672]{1,0:T(8,128)S(1)}, u32[]{:S(2)}) copy-start(f32[96,672]{1,0:T(8,128)S(1)} %fusion.22) | copy-start | bytes 774148
  394.0 22.1 %copy-start.2 = (f32[672,672]{1,0:T(8,128)S(1)}, f32[672,672]{1,0:T(8,128)}, u32[]{:S(2)}) copy-start(f32[672,672]{1,0:T(8,128)} %all-reduce.8.cloned.1.call-done) | copy-start | bytes 5419012
  436.6 10.5 %copy-start.4 = (f32[96,672]{1,0:T(8,128)}, f32[96,672]{1,0:T(8,128)S(1)}, u32[]{:S(2)}) copy-start(f32[96,672]{1,0:T(8,128)S(1)} %fusion.17) | copy-start | bytes 774148
Sparse Core Ops, SparseCore 0:
  25.4 64.3 all-reduce.3
  92.3 84.2 all-reduce.5
  260.9 133.0 all-reduce.7
